TPU v7x, 512 devices: a whole 4x8x8 slice. The times are simulated.
512 devices in a mesh: gx: 32 (over z_hi, x, core), gy: 16 (over y, z_lo).
Axes of the slice: x: 4, y: 8, z: 8 (z_hi: 4, z_lo: 2; z = z_hi * 2 + z_lo), core: 2. Of those that a mesh axis runs over, the one named last changes fastest.
Arguments:
- populations: float32 [19, 256, 256, 128], P(None, 'gx', 'gy')
- anchor: int32 [32, 16, 1024], P('gx', 'gy'), may hold values from 0 to 20606, as said below
- offsets: float32 [32, 16, 3, 1024], P('gx', 'gy'), may hold values from 0 to 0.999
- heading: float32 [32, 16, 2, 1024], P('gx', 'gy'), may hold values from -3.140625 to 3.140625
- velocity: float32 [32, 16, 3, 1024], P('gx', 'gy'), may hold values from -0.6 to 0.6
- live_count: int32 [32, 16], P('gx', 'gy'), may hold values from 1 to 1024, as said below
Outputs:
- populations_next: float32 [19, 256, 256, 128], P(None, 'gx', 'gy')
- swimmer_force: float32 [32, 16, 3, 1024], P('gx', 'gy')
Inputs may be any that keep to these rules, and one draw needn't show every extreme that they name: The anchor is (ax (18) + ay) * 128 + az with 0 <= ax <= 8, 0 <= ay <= 16, 0 <= az <= 126. Live swimmers fill slots 0 to live_count - 1 of their device; some device holds 1024.
All inputs are finite; a program needn't handle non-finite values.
Results may differ from a plain program's by a relative error of at most 0.0003.
Values sent between devices are 32-bit elements; how exact they have to be, the bound alone decides.
A program may use at most 64 MiB of HBM per device.

v0:
```python
import jax
import jax.numpy as jnp
from jax import lax
from jax.sharding import PartitionSpec as P

lattice_dirs = (
    (0, 0, 0),
    (1, 0, 0),
    (-1, 0, 0),
    (0, 1, 0),
    (0, -1, 0),
    (0, 0, 1),
    (0, 0, -1),
    (1, 1, 0),
    (-1, -1, 0),
    (1, -1, 0),
    (-1, 1, 0),
    (1, 0, 1),
    (-1, 0, -1),
    (1, 0, -1),
    (-1, 0, 1),
    (0, 1, 1),
    (0, -1, -1),
    (0, 1, -1),
    (0, -1, 1),
)
lattice_weights = (1.0 / 3.0,) + (1.0 / 18.0,) * 6 + (1.0 / 36.0,) * 12
relax_time = 0.8
friction = 2.0
propulsion = 0.5
wca_energy = 0.01
floor_square = 0.8
cutoff_square = 2.0 ** (1.0 / 3.0)


def padded(value, sides, width):
    for axis, dim in sides:
        devices, length = (lax.axis_size(axis), value.shape[dim])
        up = [(i, (i + 1) % devices) for i in range(devices)]
        down = [(j, i) for i, j in up]
        last = lax.slice_in_dim(value, length - width, length, axis=dim)
        leading = lax.slice_in_dim(value, 0, width, axis=dim)
        before = lax.ppermute(last, axis, up)
        after = lax.ppermute(leading, axis, down)
        value = jnp.concatenate([before, value, after], axis=dim)
    return value


def from_behind(value, axis, by):
    devices = lax.axis_size(axis)
    return lax.ppermute(value, axis, [(i, (i + by) % devices) for i in range(devices)])


def moments(fluid):
    dirs = jnp.asarray(lattice_dirs, jnp.float32)
    density = jnp.sum(fluid, axis=0)
    momentum = jnp.einsum("qc,qxyz->cxyz", dirs, fluid, precision=lax.Precision.HIGHEST)
    return (density, momentum)


def collide(fluid, forcing):
    dirs = jnp.asarray(lattice_dirs, jnp.float32)
    density, momentum = moments(fluid)
    speed = (momentum + 0.5 * forcing) / density
    along = jnp.einsum("qc,cxyz->qxyz", dirs, speed, precision=lax.Precision.HIGHEST)
    pushed = jnp.einsum("qc,cxyz->qxyz", dirs, forcing, precision=lax.Precision.HIGHEST)
    square = jnp.sum(speed * speed, axis=0)
    dotted = jnp.sum(speed * forcing, axis=0)
    weight = jnp.asarray(lattice_weights, jnp.float32)[:, None, None, None]
    balance = weight * density * (1.0 + 3.0 * along + 4.5 * along * along - 1.5 * square)
    source = (1.0 - 0.5 / relax_time) * weight * (3.0 * (pushed - dotted) + 9.0 * along * pushed)
    return fluid - (fluid - balance) / relax_time + source


def tent_table(length, cell, fraction):
    rows = jnp.arange(length, dtype=jnp.int32)[:, None]
    lower = jnp.where(rows == cell[None, :], 1.0 - fraction[None, :], 0.0)
    upper = jnp.where(rows == cell[None, :] + 1, fraction[None, :], 0.0)
    return lower + upper


def direction(heading):
    first = heading[..., 0, :]
    second = heading[..., 1, :]
    return jnp.stack(
        [jnp.cos(first) * jnp.cos(second), jnp.sin(first) * jnp.cos(second), jnp.sin(second)],
        axis=-2,
    )


def pair_force(own, ghosts, depth):
    delta = own[:3, :, None] - ghosts[:3, None, :]
    along_z = delta[2]
    along_z = jnp.where(
        along_z > 0.5 * depth,
        along_z - depth,
        jnp.where(along_z < -0.5 * depth, along_z + depth, along_z),
    )
    delta = jnp.stack([delta[0], delta[1], along_z])
    raw = jnp.sum(delta * delta, axis=0)
    square = jnp.maximum(raw, floor_square)
    inverse = 1.0 / square
    sixth = inverse * inverse * inverse
    magnitude = 24.0 * wca_energy * (2.0 * sixth * sixth - sixth) * inverse
    keep = jnp.where(raw < cutoff_square, ghosts[3][None, :], 0.0)
    return jnp.sum(delta * (magnitude * keep)[None], axis=2)


def body(populations, anchor, offsets, heading, velocity, live_count):
    cells_x = populations.shape[1]
    cells_y = populations.shape[2]
    cells_z = populations.shape[3]
    slot_total = anchor.shape[2]
    density, momentum = moments(populations)
    speed = momentum / density
    framed = padded(speed, (("gx", 1), ("gy", 2)), 1)
    block_row = (cells_y + 2) * cells_z
    root = anchor[0, 0]
    cell_x = root // block_row
    rest = root % block_row
    cell_y = rest // cells_z
    cell_z = rest % cells_z
    local = offsets[0, 0]
    table_x = tent_table(cells_x + 2, cell_x, local[0])
    table_y = tent_table(cells_y + 2, cell_y, local[1])
    table_z = tent_table(cells_z, cell_z, local[2])
    plane_weight = table_x[:, None, :] * table_y[None, :, :]
    along_z = jnp.einsum("cxyz,zs->cxys", framed, table_z, precision=lax.Precision.HIGHEST)
    sampled = jnp.sum(along_z * plane_weight[None], axis=(1, 2))
    count = live_count[0, 0]
    slots = jnp.arange(slot_total, dtype=jnp.int32)
    live = (slots < count).astype(jnp.float32)
    drag = friction * (sampled - velocity[0, 0])
    push = propulsion * direction(heading[0, 0])
    reaction = -(drag + push) * live[None, :]
    weighted = reaction[:, None, None, :] * plane_weight[None]
    spread = jnp.einsum("cxys,zs->cxyz", weighted, table_z, precision=lax.Precision.HIGHEST)
    from_lower_x = from_behind(spread[:, cells_x + 1 : cells_x + 2], "gx", 1)
    from_upper_x = from_behind(spread[:, 0:1], "gx", -1)
    inner = spread[:, 1 : cells_x + 1]
    inner = jnp.concatenate(
        [
            inner[:, 0:1] + from_lower_x,
            inner[:, 1 : cells_x - 1],
            inner[:, cells_x - 1 : cells_x] + from_upper_x,
        ],
        axis=1,
    )
    from_lower_y = from_behind(inner[:, :, cells_y + 1 : cells_y + 2], "gy", 1)
    from_upper_y = from_behind(inner[:, :, 0:1], "gy", -1)
    forcing = inner[:, :, 1 : cells_y + 1]
    forcing = jnp.concatenate(
        [
            forcing[:, :, 0:1] + from_lower_y,
            forcing[:, :, 1 : cells_y - 1],
            forcing[:, :, cells_y - 1 : cells_y] + from_upper_y,
        ],
        axis=2,
    )
    post = collide(populations, forcing)
    plus_x = [q for q in range(19) if lattice_dirs[q][0] == 1]
    minus_x = [q for q in range(19) if lattice_dirs[q][0] == -1]
    plus_y = [q for q in range(19) if lattice_dirs[q][1] == 1]
    minus_y = [q for q in range(19) if lattice_dirs[q][1] == -1]
    east = from_behind(jnp.stack([post[q, cells_x - 1 : cells_x] for q in plus_x]), "gx", 1)
    west = from_behind(jnp.stack([post[q, 0:1] for q in minus_x]), "gx", -1)
    section = []
    for q in range(19):
        if q in plus_x:
            section.append(jnp.concatenate([east[plus_x.index(q)], post[q, :-1]], axis=0))
        elif q in minus_x:
            section.append(jnp.concatenate([post[q, 1:], west[minus_x.index(q)]], axis=0))
        else:
            section.append(post[q])
    north = from_behind(jnp.stack([section[q][:, cells_y - 1 : cells_y] for q in plus_y]), "gy", 1)
    south = from_behind(jnp.stack([section[q][:, 0:1] for q in minus_y]), "gy", -1)
    result = []
    for q in range(19):
        if q in plus_y:
            plane = jnp.concatenate([north[plus_y.index(q)], section[q][:, :-1]], axis=1)
        elif q in minus_y:
            plane = jnp.concatenate([section[q][:, 1:], south[minus_y.index(q)]], axis=1)
        else:
            plane = section[q]
        result.append(jnp.roll(plane, lattice_dirs[q][2], axis=2))
    moved = jnp.stack(result)
    place_x = cell_x.astype(jnp.float32) - 1.0 + local[0]
    place_y = cell_y.astype(jnp.float32) - 1.0 + local[1]
    place_z = cell_z.astype(jnp.float32) + local[2]
    own = jnp.stack([place_x, place_y, place_z, live])
    beside_all = padded(own[None, None], (("gx", 0), ("gy", 1)), 1)
    step_rows = jnp.arange(3, dtype=jnp.float32) - 1.0
    shift_x = jnp.broadcast_to(step_rows[:, None] * cells_x, (3, 3))
    shift_y = jnp.broadcast_to(step_rows[None, :] * cells_y, (3, 3))
    zeros = jnp.zeros((3, 3), jnp.float32)
    moved_by = jnp.stack([shift_x, shift_y, zeros, zeros], axis=2)[:, :, :, None]
    beside_all = beside_all + moved_by
    ghosts = jnp.transpose(beside_all.reshape(9, 4, slot_total), (1, 0, 2)).reshape(
        4, 9 * slot_total
    )
    depth = jnp.float32(cells_z)
    block_rows = min(64, slot_total)
    block_count = (count + block_rows - 1) // block_rows

    def one_block(number, gathered):
        rows = lax.dynamic_slice_in_dim(own, number * block_rows, block_rows, 1)
        return lax.dynamic_update_slice_in_dim(
            gathered, pair_force(rows, ghosts, depth), number * block_rows, 1
        )

    pairs = lax.fori_loop(0, block_count, one_block, jnp.zeros((3, slot_total), jnp.float32))
    force = (pairs + drag + push) * live[None, :]
    return (moved, force.reshape(1, 1, 3, slot_total))


def solution(mesh):
    return jax.shard_map(
        body,
        mesh=mesh,
        in_specs=(
            P(None, "gx", "gy", None),
            P("gx", "gy", None),
            P("gx", "gy", None, None),
            P("gx", "gy", None, None),
            P("gx", "gy", None, None),
            P("gx", "gy"),
        ),
        out_specs=(P(None, "gx", "gy", None), P("gx", "gy", None, None)),
        check_vma=False,
    )
```

profile of v0, /device:TPU:304, one launch (start us, length us, event | category | flops | bytes accessed | tf_op | source)
XLA Modules:
  0.0 169.3 jit_solution(4191262410261082028)
XLA Ops:
  1.4 0.8 bitcast_add_fusion
  2.3 1.9 %collective-permute-start.12 = (f32[1,1,4,1024]{3,2,1,0:T(4,128)S(1)}, f32[1,1,4,1024]{3,2,1,0:T(4,128)S(1)}, u32[]{:S(2)}, u32[]{:S(2)}) collective-permute-start(f32[1,1,4,1024]{3,2,1,0:T(4,128)S(1)} %get-tuple-element.153), channel_id=1, source_target_pairs={{0,16},{16,32},{32,48},{48,64},{64,80},{80,96},{96,112},{112,128},... | collective-permute-start | bytes 49160 | tf_op jit(solution)/shard_map/ppermute | solution.py:43
  4.2 7.9 %collective-permute-start.13 = (f32[1,1,4,1024]{3,2,1,0:T(4,128)S(1)}, f32[1,1,4,1024]{3,2,1,0:T(4,128)S(1)}, u32[]{:S(2)}, u32[]{:S(2)}) collective-permute-start(f32[1,1,4,1024]{3,2,1,0:T(4,128)S(1)} %get-tuple-element.153), channel_id=1, source_target_pairs={{16,0},{32,16},{48,32},{64,48},{80,64},{96,80},{112,96},{128,112},... | collective-permute-start | bytes 49160 | tf_op jit(solution)/shard_map/ppermute | solution.py:44
  12.1 1.4 reduce_sum.64
  13.5 1.6 broadcast_divide_fusion
  15.1 1.9 %collective-permute-start = (f32[3,1,16,128]{3,0,2,1:T(4,128)S(1)}, f32[3,1,16,128]{3,0,2,1:T(4,128)S(1)}, u32[]{:S(2)}, u32[]{:S(2)}) collective-permute-start(f32[3,1,16,128]{3,0,2,1:T(4,128)S(1)} %get-tuple-element.129), channel_id=1, source_target_pairs={{0,16},{16,32},{32,48},{48,64},{64,80},{80,96},{96,112},{112,128},... | collective-permute-start | bytes 73736 | tf_op jit(solution)/shard_map/ppermute | solution.py:43
  17.1 7.9 %collective-permute-start.1 = (f32[3,1,16,128]{3,0,2,1:T(4,128)S(1)}, f32[3,1,16,128]{3,0,2,1:T(4,128)S(1)}, u32[]{:S(2)}, u32[]{:S(2)}) collective-permute-start(f32[3,1,16,128]{3,0,2,1:T(4,128)S(1)} %get-tuple-element.130), channel_id=1, source_target_pairs={{16,0},{32,16},{48,32},{64,48},{80,64},{96,80},{112,96},{128,112},... | collective-permute-start | bytes 73736 | tf_op jit(solution)/shard_map/ppermute | solution.py:44
  25.8 0.7 collective-permute-done.1
  26.5 3.5 %collective-permute-start.2 = (f32[3,10,1,128]{3,0,2,1:T(4,128)S(1)}, f32[3,10,1,128]{3,0,2,1:T(4,128)S(1)}, u32[]{:S(2)}, u32[]{:S(2)}) collective-permute-start(f32[3,10,1,128]{3,0,2,1:T(4,128)S(1)} %get-tuple-element.125), channel_id=1, source_target_pairs={{0,1},{1,2},{2,3},{3,4},{4,5},{5,6},{6,7},{7,8},{8,9},{9,10},{10,1... | collective-permute-start | bytes 46088 | tf_op jit(solution)/shard_map/ppermute | solution.py:43
  30.0 3.3 %collective-permute-start.3 = (f32[3,10,1,128]{3,0,2,1:T(4,128)S(1)}, f32[3,10,1,128]{3,0,2,1:T(4,128)S(1)}, u32[]{:S(2)}, u32[]{:S(2)}) collective-permute-start(f32[3,10,1,128]{3,0,2,1:T(4,128)S(1)} %get-tuple-element.126), channel_id=1, source_target_pairs={{1,0},{2,1},{3,2},{4,3},{5,4},{6,5},{7,6},{8,7},{9,8},{10,9},{11,1... | collective-permute-start | bytes 46088 | tf_op jit(solution)/shard_map/ppermute | solution.py:44
  33.3 2.6 %collective-permute-start.14 = (f32[3,1,4,1024]{3,2,1,0:T(4,128)S(1)}, f32[3,1,4,1024]{3,2,1,0:T(4,128)S(1)}, u32[]{:S(2)}, u32[]{:S(2)}) collective-permute-start(f32[3,1,4,1024]{3,2,1,0:T(4,128)S(1)} %pad_maximum_fusion.17), channel_id=1, source_target_pairs={{0,1},{1,2},{2,3},{3,4},{4,5},{5,6},{6,7},{7,8},{8,9},{9,10},{10,1... | collective-permute-start | bytes 147464 | tf_op jit(solution)/shard_map/ppermute | solution.py:43
  35.9 4.2 %collective-permute-start.15 = (f32[3,1,4,1024]{3,2,1,0:T(4,128)S(1)}, f32[3,1,4,1024]{3,2,1,0:T(4,128)S(1)}, u32[]{:S(2)}, u32[]{:S(2)}) collective-permute-start(f32[3,1,4,1024]{3,2,1,0:T(4,128)S(1)} %pad_maximum_fusion.17), channel_id=1, source_target_pairs={{1,0},{2,1},{3,2},{4,3},{5,4},{6,5},{7,6},{8,7},{9,8},{10,9},{11,1... | collective-permute-start | bytes 147464 | tf_op jit(solution)/shard_map/ppermute | solution.py:44
  40.2 2.6 %multiply_reduce_fusion.2 = f32[3,1024]{1,0:T(4,128)S(1)} fusion(f32[10,18,1024]{2,1,0:T(8,128)S(1)} %broadcast_multiply_fusion, f32[3,10,18,128]{3,0,2,1:T(4,128)S(1)} %pad_maximum_fusion.1, f32[1024]{0:T(1024)S(1)} %bitcast.295, s32[1024]{0:T(1024)S(1)} %get-tuple-element.86, f32[1024]{0:T(1024)S(1)} %broadcast_subtract_fusion.3, ...), kind=kOutput, calls=%fused_computation.14 | convolution fusion | flops 851104768 | bytes 1042432 | tf_op jit(solution)/shard_map/cxyz,zs->cxys/dot_general | solution.py:128
  43.1 21.0 %while.12 = (s32[]{:T(128)}, f32[3,1024]{1,0:T(4,128)S(1)}, s32[]{:T(128)}, f32[4,1024]{1,0:T(4,128)S(1)}, f32[4,9216]{1,0:T(4,128)S(1)}, /*index=5*/s32[]{:T(128)}, s32[]{:T(128)}, s32[]{:T(128)}, s32[]{:T(128)}) while((s32[]{:T(128)}, f32[3,1024]{1,0:T(4,128)S(1)}, s32[]{:T(128)}, f32[4,1024]{1,0:T(4,128)S(1)}, f32[4,9216]{1,0:T(4,128)S(1)}, ...), condition=%wide.region_7.8_spmd, body=%wide.region_4.7_spmd.sunk | while | flops 22413124 | bytes 45053076 | solution.py:211
  43.2 0.8 broadcast_subtract_fusion.5
  44.0 0.3 slice.700
  44.3 0.5 fusion.80
  44.8 0.7 multiply_reduce_fusion.7
  45.5 0.9 fusion.81
  46.5 0.7 multiply_reduce_fusion.8
  47.3 0.8 broadcast_subtract_fusion.5
  48.1 0.3 slice.700
  48.5 0.5 fusion.80
  48.9 0.7 multiply_reduce_fusion.7
  49.7 0.9 fusion.81
  50.6 0.7 multiply_reduce_fusion.8
  51.5 0.8 broadcast_subtract_fusion.5
  52.3 0.3 slice.700
  52.7 0.5 fusion.80
  53.1 0.7 multiply_reduce_fusion.7
  53.9 0.9 fusion.81
  54.8 0.7 multiply_reduce_fusion.8
  55.7 0.8 broadcast_subtract_fusion.5
  56.5 0.3 slice.700
  56.8 0.5 fusion.80
  57.3 0.7 multiply_reduce_fusion.7
  58.0 0.9 fusion.81
  58.9 0.7 multiply_reduce_fusion.8
  59.9 0.8 broadcast_subtract_fusion.5
  60.7 0.3 slice.700
  61.0 0.5 fusion.80
  61.5 0.7 multiply_reduce_fusion.7
  62.2 0.9 fusion.81
  63.2 0.7 multiply_reduce_fusion.8
  64.2 2.5 %fusion.4 = f32[3,10,18,128]{3,2,1,0:T(8,128)S(1)} fusion(f32[3,1024]{1,0:T(4,128)S(1)} %get-tuple-element.132, f32[10,18,1024]{2,1,0:T(8,128)S(1)} %broadcast_multiply_fusion, f32[1024]{0:T(1024)S(1)} %bitcast.296, s32[1024]{0:T(1024)S(1)} %get-tuple-element.86, f32[1024]{0:T(1024)S(1)} %broadcast_subtract_fusion.3, s32[1024]{0:T(1024)S(1)} %get-tuple-element.87), kind=kOutput, calls=%fused_computation.12 | convolution fusion | flops 850554880 | bytes 1042432 | tf_op jit(solution)/shard_map/cxys,zs->cxyz/dot_general | solution.py:137
  66.7 7.2 %collective-permute-start.4 = (f32[3,1,18,128]{3,0,2,1:T(4,128)S(1)}, f32[3,1,18,128]{3,0,2,1:T(4,128)S(1)}, u32[]{:S(2)}, u32[]{:S(2)}) collective-permute-start(f32[3,1,18,128]{3,0,2,1:T(4,128)S(1)} %copy.201), channel_id=1, source_target_pairs={{0,16},{16,32},{32,48},{48,64},{64,80},{80,96},{96,112},{112,128},... | collective-permute-start | bytes 82952 | tf_op jit(solution)/shard_map/ppermute | solution.py:51
  74.1 2.5 %collective-permute-start.5 = (f32[3,1,18,128]{3,0,2,1:T(4,128)S(1)}, f32[3,1,18,128]{3,0,2,1:T(4,128)S(1)}, u32[]{:S(2)}, u32[]{:S(2)}) collective-permute-start(f32[3,1,18,128]{3,0,2,1:T(4,128)S(1)} %copy.204), channel_id=1, source_target_pairs={{0,496},{16,0},{32,16},{48,32},{64,48},{80,64},{96,80},{112,96},{1... | collective-permute-start | bytes 82952 | tf_op jit(solution)/shard_map/ppermute | solution.py:51
  76.6 1.6 collective-permute-done.5
  78.3 11.7 %collective-permute-start.6 = (f32[3,8,1,128]{3,0,2,1:T(4,128)S(1)}, f32[3,8,1,128]{3,0,2,1:T(4,128)S(1)}, u32[]{:S(2)}, u32[]{:S(2)}) collective-permute-start(f32[3,8,1,128]{3,0,2,1:T(4,128)S(1)} %pad_maximum_fusion.22), channel_id=1, source_target_pairs={{0,1},{1,2},{2,3},{3,4},{4,5},{5,6},{6,7},{7,8},{8,9},{9,10},{10,1... | collective-permute-start | bytes 36872 | tf_op jit(solution)/shard_map/ppermute | solution.py:51
  89.9 0.6 reshape.571
  90.6 39.4 %collective-permute-done.6 = f32[3,8,1,128]{3,0,2,1:T(4,128)S(1)} collective-permute-done((f32[3,8,1,128]{3,0,2,1:T(4,128)S(1)}, f32[3,8,1,128]{3,0,2,1:T(4,128)S(1)}, u32[]{:S(2)}, u32[]{:S(2)}) %collective-permute-start.6) | collective-permute-done | bytes 12320 | tf_op jit(solution)/shard_map/ppermute | solution.py:51
  130.0 3.9 %collective-permute-start.7 = (f32[3,8,1,128]{3,0,2,1:T(4,128)S(1)}, f32[3,8,1,128]{3,0,2,1:T(4,128)S(1)}, u32[]{:S(2)}, u32[]{:S(2)}) collective-permute-start(f32[3,8,1,128]{3,0,2,1:T(4,128)S(1)} %get-tuple-element.128), channel_id=1, source_target_pairs={{0,15},{1,0},{2,1},{3,2},{4,3},{5,4},{6,5},{7,6},{8,7},{9,8},{10,9... | collective-permute-start | bytes 36872 | tf_op jit(solution)/shard_map/ppermute | solution.py:51
  134.1 1.6 collective-permute-done.7
  135.6 1.5 fusion.67
  137.1 0.4 multiply_reduce_fusion.4
  137.6 1.5 fusion.73
  139.1 0.8 fusion.16
  140.1 5.8 %collective-permute-start.9 = (f32[5,1,16,128]{3,2,1,0:T(8,128)S(1)}, f32[5,1,16,128]{3,2,1,0:T(8,128)S(1)}, u32[]{:S(2)}, u32[]{:S(2)}) collective-permute-start(f32[5,1,16,128]{3,2,1,0:T(8,128)S(1)} %get-tuple-element.111), channel_id=1, source_target_pairs={{0,496},{16,0},{32,16},{48,32},{64,48},{80,64},{96,80},{112,96},{1... | collective-permute-start | bytes 122888 | tf_op jit(solution)/shard_map/ppermute | solution.py:51
  146.1 1.9 %collective-permute-start.8 = (f32[5,1,16,128]{3,2,1,0:T(8,128)S(1)}, f32[5,1,16,128]{3,2,1,0:T(8,128)S(1)}, u32[]{:S(2)}, u32[]{:S(2)}) collective-permute-start(f32[5,1,16,128]{3,2,1,0:T(8,128)S(1)} %get-tuple-element.112), channel_id=1, source_target_pairs={{0,16},{16,32},{32,48},{48,64},{64,80},{80,96},{96,112},{112,128},... | collective-permute-start | bytes 122888 | tf_op jit(solution)/shard_map/ppermute | solution.py:51
  148.5 7.1 %collective-permute-done.8 = f32[5,1,16,128]{3,2,1,0:T(8,128)S(1)} collective-permute-done((f32[5,1,16,128]{3,2,1,0:T(8,128)S(1)}, f32[5,1,16,128]{3,2,1,0:T(8,128)S(1)}, u32[]{:S(2)}, u32[]{:S(2)}) %collective-permute-start.8) | collective-permute-done | bytes 40992 | tf_op jit(solution)/shard_map/ppermute | solution.py:51
  155.6 4.5 %collective-permute-start.11 = (f32[5,8,1,128]{3,1,2,0:T(8,128)S(1)}, f32[5,8,1,128]{3,1,2,0:T(8,128)S(1)}, u32[]{:S(2)}, u32[]{:S(2)}) collective-permute-start(f32[5,8,1,128]{3,1,2,0:T(8,128)S(1)} %constant_dynamic-update-slice_fusion.15), channel_id=1, source_target_pairs={{0,15},{1,0},{2,1},{3,2},{4,3},{5,4},{6,5},{7,6},{8,7},{9,8},{10,9... | collective-permute-start | bytes 61448 | tf_op jit(solution)/shard_map/ppermute | solution.py:51
  160.2 1.9 %collective-permute-start.10 = (f32[5,8,1,128]{3,1,2,0:T(8,128)S(1)}, f32[5,8,1,128]{3,1,2,0:T(8,128)S(1)}, u32[]{:S(2)}, u32[]{:S(2)}) collective-permute-start(f32[5,8,1,128]{3,1,2,0:T(8,128)S(1)} %constant_dynamic-update-slice_fusion.10), channel_id=1, source_target_pairs={{0,1},{1,2},{2,3},{3,4},{4,5},{5,6},{6,7},{7,8},{8,9},{9,10},{10,1... | collective-permute-start | bytes 61448 | tf_op jit(solution)/shard_map/ppermute | solution.py:51
  162.7 4.1 %collective-permute-done.10 = f32[5,8,1,128]{3,1,2,0:T(8,128)S(1)} collective-permute-done((f32[5,8,1,128]{3,1,2,0:T(8,128)S(1)}, f32[5,8,1,128]{3,1,2,0:T(8,128)S(1)}, u32[]{:S(2)}, u32[]{:S(2)}) %collective-permute-start.10) | collective-permute-done | bytes 20512 | tf_op jit(solution)/shard_map/ppermute | solution.py:51
  168.2 1.0 copy-done.6
  (157 shorter events, 5.2 us)
Async XLA Ops:
  0.6 12.8 %copy-start.3 = (f32[19,3,1,1]{0,1,3,2:T(4,128)S(1)}, f32[19,3,1,1]{0,1,3,2:T(4,128)}, u32[]{:S(2)}) copy-start(f32[19,3,1,1]{0,1,3,2:T(4,128)} %constant.175) | copy-start | bytes 688
  0.6 12.8 %copy-start = (f32[19,8,16,128]{3,2,1,0:T(8,128)S(1)}, f32[19,8,16,128]{3,2,1,0:T(8,128)}, u32[]{:S(2)}) copy-start(f32[19,8,16,128]{3,2,1,0:T(8,128)} %param.12) | copy-start | bytes 3735556
  2.3 31.0 %collective-permute-start.12 = (f32[1,1,4,1024]{3,2,1,0:T(4,128)S(1)}, f32[1,1,4,1024]{3,2,1,0:T(4,128)S(1)}, u32[]{:S(2)}, u32[]{:S(2)}) collective-permute-start(f32[1,1,4,1024]{3,2,1,0:T(4,128)S(1)} %get-tuple-element.153), channel_id=1, source_target_pairs={{0,16},{16,32},{32,48},{48,64},{64,80},{80,96},{96,112},{112,128},... | collective-permute-start | bytes 49160 | tf_op jit(solution)/shard_map/ppermute | solution.py:43
  4.2 29.1 %collective-permute-start.13 = (f32[1,1,4,1024]{3,2,1,0:T(4,128)S(1)}, f32[1,1,4,1024]{3,2,1,0:T(4,128)S(1)}, u32[]{:S(2)}, u32[]{:S(2)}) collective-permute-start(f32[1,1,4,1024]{3,2,1,0:T(4,128)S(1)} %get-tuple-element.153), channel_id=1, source_target_pairs={{16,0},{32,16},{48,32},{64,48},{80,64},{96,80},{112,96},{128,112},... | collective-permute-start | bytes 49160 | tf_op jit(solution)/shard_map/ppermute | solution.py:44
  13.5 11.5 %copy-start.2 = (s32[1,1,1024]{2,1,0:T(1,128)S(1)}, s32[1,1,1024]{2,1,0:T(1,128)}, u32[]{:S(2)}) copy-start(s32[1,1,1024]{2,1,0:T(1,128)} %param.13) | copy-start | bytes 12292
  13.5 11.6 %copy-start.1 = (f32[1,1,3,1024]{3,1,2,0:T(1,128)S(1)}, f32[1,1,3,1024]{3,1,2,0:T(1,128)}, u32[]{:S(2)}) copy-start(f32[1,1,3,1024]{3,1,2,0:T(1,128)} %param.14) | copy-start | bytes 36868
  13.5 11.6 %copy-start.5 = (f32[1,1,2,1024]{3,2,1,0:T(2,128)S(1)}, f32[1,1,2,1024]{3,2,1,0:T(2,128)}, u32[]{:S(2)}) copy-start(f32[1,1,2,1024]{3,2,1,0:T(2,128)} %param.15) | copy-start | bytes 24580
  15.1 10.7 %collective-permute-start = (f32[3,1,16,128]{3,0,2,1:T(4,128)S(1)}, f32[3,1,16,128]{3,0,2,1:T(4,128)S(1)}, u32[]{:S(2)}, u32[]{:S(2)}) collective-permute-start(f32[3,1,16,128]{3,0,2,1:T(4,128)S(1)} %get-tuple-element.129), channel_id=1, source_target_pairs={{0,16},{16,32},{32,48},{48,64},{64,80},{80,96},{96,112},{112,128},... | collective-permute-start | bytes 73736 | tf_op jit(solution)/shard_map/ppermute | solution.py:43
  17.1 9.4 %collective-permute-start.1 = (f32[3,1,16,128]{3,0,2,1:T(4,128)S(1)}, f32[3,1,16,128]{3,0,2,1:T(4,128)S(1)}, u32[]{:S(2)}, u32[]{:S(2)}) collective-permute-start(f32[3,1,16,128]{3,0,2,1:T(4,128)S(1)} %get-tuple-element.130), channel_id=1, source_target_pairs={{16,0},{32,16},{48,32},{64,48},{80,64},{96,80},{112,96},{128,112},... | collective-permute-start | bytes 73736 | tf_op jit(solution)/shard_map/ppermute | solution.py:44
  26.5 13.6 %collective-permute-start.2 = (f32[3,10,1,128]{3,0,2,1:T(4,128)S(1)}, f32[3,10,1,128]{3,0,2,1:T(4,128)S(1)}, u32[]{:S(2)}, u32[]{:S(2)}) collective-permute-start(f32[3,10,1,128]{3,0,2,1:T(4,128)S(1)} %get-tuple-element.125), channel_id=1, source_target_pairs={{0,1},{1,2},{2,3},{3,4},{4,5},{5,6},{6,7},{7,8},{8,9},{9,10},{10,1... | collective-permute-start | bytes 46088 | tf_op jit(solution)/shard_map/ppermute | solution.py:43
  30.0 10.1 %collective-permute-start.3 = (f32[3,10,1,128]{3,0,2,1:T(4,128)S(1)}, f32[3,10,1,128]{3,0,2,1:T(4,128)S(1)}, u32[]{:S(2)}, u32[]{:S(2)}) collective-permute-start(f32[3,10,1,128]{3,0,2,1:T(4,128)S(1)} %get-tuple-element.126), channel_id=1, source_target_pairs={{1,0},{2,1},{3,2},{4,3},{5,4},{6,5},{7,6},{8,7},{9,8},{10,9},{11,1... | collective-permute-start | bytes 46088 | tf_op jit(solution)/shard_map/ppermute | solution.py:44
  33.3 9.5 %collective-permute-start.14 = (f32[3,1,4,1024]{3,2,1,0:T(4,128)S(1)}, f32[3,1,4,1024]{3,2,1,0:T(4,128)S(1)}, u32[]{:S(2)}, u32[]{:S(2)}) collective-permute-start(f32[3,1,4,1024]{3,2,1,0:T(4,128)S(1)} %pad_maximum_fusion.17), channel_id=1, source_target_pairs={{0,1},{1,2},{2,3},{3,4},{4,5},{5,6},{6,7},{7,8},{8,9},{9,10},{10,1... | collective-permute-start | bytes 147464 | tf_op jit(solution)/shard_map/ppermute | solution.py:43
  35.9 6.9 %collective-permute-start.15 = (f32[3,1,4,1024]{3,2,1,0:T(4,128)S(1)}, f32[3,1,4,1024]{3,2,1,0:T(4,128)S(1)}, u32[]{:S(2)}, u32[]{:S(2)}) collective-permute-start(f32[3,1,4,1024]{3,2,1,0:T(4,128)S(1)} %pad_maximum_fusion.17), channel_id=1, source_target_pairs={{1,0},{2,1},{3,2},{4,3},{5,4},{6,5},{7,6},{8,7},{9,8},{10,9},{11,1... | collective-permute-start | bytes 147464 | tf_op jit(solution)/shard_map/ppermute | solution.py:44
  43.1 21.0 %copy-start.4 = (f32[1,1,3,1024]{3,1,2,0:T(1,128)S(1)}, f32[1,1,3,1024]{3,1,2,0:T(1,128)}, u32[]{:S(2)}) copy-start(f32[1,1,3,1024]{3,1,2,0:T(1,128)} %param.16) | copy-start | bytes 36868
  66.7 9.9 %collective-permute-start.4 = (f32[3,1,18,128]{3,0,2,1:T(4,128)S(1)}, f32[3,1,18,128]{3,0,2,1:T(4,128)S(1)}, u32[]{:S(2)}, u32[]{:S(2)}) collective-permute-start(f32[3,1,18,128]{3,0,2,1:T(4,128)S(1)} %copy.201), channel_id=1, source_target_pairs={{0,16},{16,32},{32,48},{48,64},{64,80},{80,96},{96,112},{112,128},... | collective-permute-start | bytes 82952 | tf_op jit(solution)/shard_map/ppermute | solution.py:51
  74.1 4.2 %collective-permute-start.5 = (f32[3,1,18,128]{3,0,2,1:T(4,128)S(1)}, f32[3,1,18,128]{3,0,2,1:T(4,128)S(1)}, u32[]{:S(2)}, u32[]{:S(2)}) collective-permute-start(f32[3,1,18,128]{3,0,2,1:T(4,128)S(1)} %copy.204), channel_id=1, source_target_pairs={{0,496},{16,0},{32,16},{48,32},{64,48},{80,64},{96,80},{112,96},{1... | collective-permute-start | bytes 82952 | tf_op jit(solution)/shard_map/ppermute | solution.py:51
  78.3 51.7 %collective-permute-start.6 = (f32[3,8,1,128]{3,0,2,1:T(4,128)S(1)}, f32[3,8,1,128]{3,0,2,1:T(4,128)S(1)}, u32[]{:S(2)}, u32[]{:S(2)}) collective-permute-start(f32[3,8,1,128]{3,0,2,1:T(4,128)S(1)} %pad_maximum_fusion.22), channel_id=1, source_target_pairs={{0,1},{1,2},{2,3},{3,4},{4,5},{5,6},{6,7},{7,8},{8,9},{9,10},{10,1... | collective-permute-start | bytes 36872 | tf_op jit(solution)/shard_map/ppermute | solution.py:51
  130.0 5.6 %collective-permute-start.7 = (f32[3,8,1,128]{3,0,2,1:T(4,128)S(1)}, f32[3,8,1,128]{3,0,2,1:T(4,128)S(1)}, u32[]{:S(2)}, u32[]{:S(2)}) collective-permute-start(f32[3,8,1,128]{3,0,2,1:T(4,128)S(1)} %get-tuple-element.128), channel_id=1, source_target_pairs={{0,15},{1,0},{2,1},{3,2},{4,3},{5,4},{6,5},{7,6},{8,7},{9,8},{10,9... | collective-permute-start | bytes 36872 | tf_op jit(solution)/shard_map/ppermute | solution.py:51
  137.1 1.9 %copy-start.7 = (f32[19]{0:T(128)S(1)}, f32[19]{0:T(128)}, u32[]{:S(2)}) copy-start(f32[19]{0:T(128)} %constant.167.clone) | copy-start | bytes 232
  137.1 1.9 %copy-start.8 = (f32[19]{0:T(128)S(1)}, f32[19]{0:T(128)}, u32[]{:S(2)}) copy-start(f32[19]{0:T(128)} %constant.174) | copy-start | bytes 232
  140.1 8.3 %collective-permute-start.9 = (f32[5,1,16,128]{3,2,1,0:T(8,128)S(1)}, f32[5,1,16,128]{3,2,1,0:T(8,128)S(1)}, u32[]{:S(2)}, u32[]{:S(2)}) collective-permute-start(f32[5,1,16,128]{3,2,1,0:T(8,128)S(1)} %get-tuple-element.111), channel_id=1, source_target_pairs={{0,496},{16,0},{32,16},{48,32},{64,48},{80,64},{96,80},{112,96},{1... | collective-permute-start | bytes 122888 | tf_op jit(solution)/shard_map/ppermute | solution.py:51
  146.1 9.5 %collective-permute-start.8 = (f32[5,1,16,128]{3,2,1,0:T(8,128)S(1)}, f32[5,1,16,128]{3,2,1,0:T(8,128)S(1)}, u32[]{:S(2)}, u32[]{:S(2)}) collective-permute-start(f32[5,1,16,128]{3,2,1,0:T(8,128)S(1)} %get-tuple-element.112), channel_id=1, source_target_pairs={{0,16},{16,32},{32,48},{48,64},{64,80},{80,96},{96,112},{112,128},... | collective-permute-start | bytes 122888 | tf_op jit(solution)/shard_map/ppermute | solution.py:51
  155.6 6.9 %collective-permute-start.11 = (f32[5,8,1,128]{3,1,2,0:T(8,128)S(1)}, f32[5,8,1,128]{3,1,2,0:T(8,128)S(1)}, u32[]{:S(2)}, u32[]{:S(2)}) collective-permute-start(f32[5,8,1,128]{3,1,2,0:T(8,128)S(1)} %constant_dynamic-update-slice_fusion.15), channel_id=1, source_target_pairs={{0,15},{1,0},{2,1},{3,2},{4,3},{5,4},{6,5},{7,6},{8,7},{9,8},{10,9... | collective-permute-start | bytes 61448 | tf_op jit(solution)/shard_map/ppermute | solution.py:51
  160.2 6.6 %collective-permute-start.10 = (f32[5,8,1,128]{3,1,2,0:T(8,128)S(1)}, f32[5,8,1,128]{3,1,2,0:T(8,128)S(1)}, u32[]{:S(2)}, u32[]{:S(2)}) collective-permute-start(f32[5,8,1,128]{3,1,2,0:T(8,128)S(1)} %constant_dynamic-update-slice_fusion.10), channel_id=1, source_target_pairs={{0,1},{1,2},{2,3},{3,4},{4,5},{5,6},{6,7},{7,8},{8,9},{9,10},{10,1... | collective-permute-start | bytes 61448 | tf_op jit(solution)/shard_map/ppermute | solution.py:51
  168.2 1.0 copy-start.6
where the time goes:
time: 166 us; the launch traced here: 169 us
  starting transfers between devices  72.7 us (44%)
  waiting for transfers between devices  54.5 us (33%)
  other arithmetic  23.7 us (14%)
  matrix products  9.63 us (6%)
  local copies, waits for them, and re-layouts  5.76 us (3%)
  between operations  2.46 us (1%)
    ppermute x8, waiting for transfers between devices, from_behind(): lax.ppermute(value, axis, [(i, (i + by) % devices) for i in range(devices)])  53.8 us
    ppermute x8, starting transfers between devices, from_behind(): lax.ppermute(value, axis, [(i, (i + by) % devices) for i in range(devices)])  39.6 us
    ppermute x4, starting transfers between devices, padded(): after = lax.ppermute(leading, axis, down)  23.2 us
    ppermute x4, starting transfers between devices, padded(): before = lax.ppermute(last, axis, up)  9.88 us
    mul x5, other arithmetic, pair_force(): return jnp.sum(delta * (magnitude * keep)[None], axis=2)  4.63 us
    sub x5, other arithmetic, pair_force(): delta = own[:3, :, None] - ghosts[:3, None, :]  3.94 us
    reduce_sum x5, other arithmetic, pair_force(): raw = jnp.sum(delta * delta, axis=0)  3.45 us
  transfers between devices with their start and end apart: 16, of which 6 were waited for; matrix products, arithmetic and copies ran while one was open for 5% of the time, Pallas kernels for 0%

commit v1 on v0

v1 whole, which is shorter than its diff:
```python
import functools

import jax
import jax.numpy as jnp
import numpy as np
from jax import lax
from jax.experimental import pallas as pl
from jax.experimental.pallas import tpu as pltpu
from jax.sharding import PartitionSpec as P

DIRS = (
    (0, 0, 0), (1, 0, 0), (-1, 0, 0), (0, 1, 0), (0, -1, 0), (0, 0, 1), (0, 0, -1),
    (1, 1, 0), (-1, -1, 0), (1, -1, 0), (-1, 1, 0), (1, 0, 1), (-1, 0, -1),
    (1, 0, -1), (-1, 0, 1), (0, 1, 1), (0, -1, -1), (0, 1, -1), (0, -1, 1),
)
WEIGHTS = (1.0 / 3.0,) + (1.0 / 18.0,) * 6 + (1.0 / 36.0,) * 12
CUTOFF = 2.0 ** (1.0 / 3.0)
REACH = 1.125
FAR = 1.0e9
F32 = jnp.float32
BF16 = jnp.bfloat16
MESH = pl.DeviceIdType.MESH

CX, CY, NZ, SW = 8, 16, 128, 1024
ROWS = CX * CY
LANE_TILES = SW // 128

SIDES = ((-1, 0), (1, 0), (0, -1), (0, 1), (-1, -1), (-1, 1), (1, -1), (1, 1))
RANGES = ((0, 4, 7), (1, 0, 3), (2, 2, 5), (3, 6, 8), (3, 0, 1), (4, 4, 5), (5, 6, 7), (6, 2, 3), (7, 0, 1))


def facing(axis, sign):
    return [q for q in range(19) if DIRS[q][axis] == sign]


def corner_q(sx, sy):
    return DIRS.index((-sx, -sy, 0))


def split2(v):
    hi = v.astype(BF16)
    return hi, (v - hi.astype(F32)).astype(BF16)


def split3(v):
    hi = v.astype(BF16)
    rest = v - hi.astype(F32)
    mid = rest.astype(BF16)
    return hi, mid, (rest - mid.astype(F32)).astype(BF16)


def dot(a, b):
    return lax.dot_general(a, b, (((1,), (0,)), ((), ())), preferred_element_type=F32)


def dot_t(a, b):
    return lax.dot_general(a, b, (((1,), (1,)), ((), ())), preferred_element_type=F32)


def tent(d):
    return jnp.maximum(1.0 - jnp.abs(d), 0.0)


def moments(load):
    rho = None
    mom = [None, None, None]
    for q in range(19):
        f = load(q)
        rho = f if rho is None else rho + f
        for c in range(3):
            s = DIRS[q][c]
            if s:
                if mom[c] is None:
                    mom[c] = f if s > 0 else -f
                else:
                    mom[c] = mom[c] + f if s > 0 else mom[c] - f
    return rho, mom


def pair_terms(ox, oy, oz, px, py, pz):
    dx = ox - px
    dy = oy - py
    dz = oz - pz
    dz = dz - NZ * jnp.round(dz * (1.0 / NZ))
    raw = dx * dx + dy * dy + dz * dz
    inv = 1.0 / jnp.maximum(raw, 0.8)
    sixth = inv * inv * inv
    mag = (sixth + sixth - 1.0) * (sixth * inv)
    mag = jnp.where(raw < CUTOFF, mag, 0.0)
    return mag * dx, mag * dy, mag * dz


def exchange_kernel(n_gx, n_gy, pops, anchor, offsets, heading, velocity, count,
                    halo_x, halo_y, halo_c, lists, starts_out, own_out, pair_out,
                    pv, msg_x, msg_y, msg_c, msg_l, msg_s, mom, cols, pop_sem, send_sem, recv_sem):
    gx = lax.axis_index("gx")
    gy = lax.axis_index("gy")

    def device(side):
        return (lax.rem(gx + side[0] + n_gx, n_gx), lax.rem(gy + side[1] + n_gy, n_gy))

    loads = [pltpu.make_async_copy(pops.at[q], pv.at[q], pop_sem.at[q]) for q in range(19)]
    for c in loads:
        c.start()
    barrier = pltpu.get_barrier_semaphore()
    for side in SIDES:
        pl.semaphore_signal(barrier, inc=1, device_id=device(side), device_id_type=MESH)

    root = anchor[0]
    bx = lax.shift_right_logical(root, 7)
    cz = root & (NZ - 1)
    bxf = bx.astype(F32)
    cxf = jnp.floor(bxf * (1.0 / (CY + 2)) + 0.01)
    cyf = bxf - cxf * (CY + 2)
    off = offsets[0, 0]
    x = cxf - 1.0 + off[0:1]
    y = cyf - 1.0 + off[1:2]
    z = cz.astype(F32) + off[2:3]
    slot = lax.broadcasted_iota(jnp.int32, (1, SW), 1)
    live = (slot < count[0, 0]).astype(F32)
    ang = heading[0, 0]
    cs, sn = jnp.cos(ang), jnp.sin(ang)
    vel = velocity[0, 0]
    c1 = cs[1:2]
    w = [2.0 * vel[0:1] - 0.5 * (cs[0:1] * c1),
         2.0 * vel[1:2] - 0.5 * (sn[0:1] * c1),
         2.0 * vel[2:3] - 0.5 * sn[1:2]]
    zero = jnp.zeros((1, SW), F32)
    table = jnp.concatenate([x, y, z, w[0], w[1], w[2], live, zero], axis=0)
    own_out[...] = table

    xl, xh = x < REACH, x > CX - 1 - REACH
    yl, yh = y < REACH, y > CY - 1 - REACH
    yc = jnp.where(yl, 0.0, jnp.where(yh, 2.0, 1.0))
    kind = jnp.where(xl, yc, jnp.where(xh, 6.0 - yc, jnp.where(yl, 7.0, jnp.where(yh, 3.0, 8.0))))
    kind = jnp.where(live > 0.0, kind, 9.0)
    krow = lax.broadcasted_iota(jnp.int32, (16, SW), 0).astype(F32)
    member = (krow == kind).astype(F32)
    stack = jnp.concatenate([member[:, t * 128:(t + 1) * 128] for t in range(LANE_TILES)], axis=0).astype(BF16)
    ri = lax.broadcasted_iota(jnp.int32, (128, 256), 0)
    ci = lax.broadcasted_iota(jnp.int32, (128, 256), 1)
    upper = ((ri < ci) | (ci >= 128)).astype(F32).astype(BF16)
    pre = dot(stack, upper)
    base = jnp.zeros((16, 128), F32)
    within = []
    for t in range(LANE_TILES):
        blk = pre[t * 16:(t + 1) * 16]
        within.append(blk[:, :128] + base)
        base = base + blk[:, 128:]
    acc = jnp.zeros((1, 128), F32)
    starts = []
    for k in range(10):
        starts.append(acc)
        acc = acc + base[k:k + 1]
    first = jnp.concatenate(starts + [acc] * 6, axis=0)
    ranks = [jnp.sum(member[:, t * 128:(t + 1) * 128] * (within[t] + first), axis=0, keepdims=True)
             for t in range(LANE_TILES)]
    lane = lax.broadcasted_iota(jnp.int32, (1, 128), 1)
    row = jnp.zeros((1, 128), F32)
    for k in range(10):
        row = jnp.where(lane == k, first[k:k + 1], row)
    msg_s[...] = jnp.broadcast_to(row, (8, 128))

    parts = jnp.concatenate(split3(table), axis=0)
    dst = lax.broadcasted_iota(jnp.int32, (SW, 128), 0).astype(F32)
    total = jnp.zeros((24, SW), F32)
    for t in range(0, LANE_TILES, 2):
        hot = jnp.concatenate([(dst == ranks[t]).astype(F32).astype(BF16),
                               (dst == ranks[t + 1]).astype(F32).astype(BF16)], axis=1)
        total = total + dot_t(parts[:, t * 128:(t + 2) * 128], hot)
    ordered = total[0:8] + total[8:16] + total[16:24]
    for t in range(LANE_TILES):
        msg_l[t] = ordered[:, t * 128:(t + 1) * 128]

    for c in loads:
        c.wait()
    rho, m = moments(lambda q: pv[q])
    inv = 1.0 / rho
    mom[0] = rho
    for c in range(3):
        mom[1 + c] = m[c] * inv
    for s, (adj, far) in enumerate(((0, 1), (CX - 1, CX - 2))):
        for c in range(4):
            msg_x[s, c] = mom[c, adj * CY:(adj + 1) * CY]
        for c in range(3):
            msg_x[s, 4 + c] = mom[1 + c, far * CY:(far + 1) * CY]
        for k, q in enumerate(facing(0, 2 * s - 1)):
            msg_x[s, 7 + k] = pv[q, adj * CY:(adj + 1) * CY]
    for s, (adj, far) in enumerate(((0, 1), (CY - 1, CY - 2))):
        for c in range(4):
            msg_y[s, c] = mom[c, pl.ds(adj, CX, stride=CY)]
        for c in range(3):
            msg_y[s, 4 + c] = mom[1 + c, pl.ds(far, CX, stride=CY)]
        for k, q in enumerate(facing(1, 2 * s - 1)):
            msg_y[s, 7 + k] = pv[q, pl.ds(adj, CX, stride=CY)]
    for i in range(4):
        sx, sy = SIDES[4 + i]
        ax, fx = (0, 1) if sx < 0 else (CX - 1, CX - 2)
        ay, fy = (0, 1) if sy < 0 else (CY - 1, CY - 2)
        msg_c[i] = jnp.zeros((16, 128), F32)
        for c in range(4):
            msg_c[i, c:c + 1] = mom[c, ax * CY + ay:ax * CY + ay + 1]
        for j, (nx, ny) in enumerate(((ax, fy), (fx, ay), (fx, fy))):
            for c in range(3):
                msg_c[i, 5 + 3 * j + c:6 + 3 * j + c] = mom[1 + c, nx * CY + ny:nx * CY + ny + 1]
        q = DIRS.index((sx, sy, 0))
        msg_c[i, 4:5] = pv[q, ax * CY + ay:ax * CY + ay + 1]

    pl.semaphore_wait(barrier, 8)
    copies = []
    for d, side in enumerate(SIDES):
        o = SIDES.index((-side[0], -side[1]))
        if side[1] == 0:
            src, out = msg_x.at[d], halo_x.at[o]
        elif side[0] == 0:
            src, out = msg_y.at[d - 2], halo_y.at[o - 2]
        else:
            src, out = msg_c.at[d - 4], halo_c.at[o - 4]
        for k, (a, b) in enumerate(((src, out), (msg_l, lists.at[o]), (msg_s, starts_out.at[o]))):
            copies.append(pltpu.make_async_remote_copy(
                src_ref=a, dst_ref=b, send_sem=send_sem.at[3 * d + k], recv_sem=recv_sem.at[3 * o + k],
                device_id=device(side), device_id_type=MESH))
    for c in copies:
        c.start()

    place = jnp.concatenate([jnp.where(live > 0.0, x, FAR), y, z, zero, zero, zero, zero, zero], axis=0)
    for t in range(LANE_TILES):
        cols_t = jnp.transpose(place[:, t * 128:(t + 1) * 128])
        for c in range(3):
            cols[c, t * 128:(t + 1) * 128] = jnp.broadcast_to(cols_t[:, c:c + 1], (128, 128))
    width = 512
    for h in range(SW // width):
        own = [jnp.broadcast_to(v[:, h * width:(h + 1) * width], (8, width)) for v in (x, y, z)]

        def step(g, carry, own=own):
            at = pl.multiple_of(g * 8, 8)
            p = [jnp.concatenate([cols[c, pl.ds(at, 8)]] * (width // 128), axis=1) for c in range(3)]
            f = pair_terms(*own, *p)
            return tuple(a + b for a, b in zip(carry, f))

        init = tuple(jnp.zeros((8, width), F32) for _ in range(3))
        got = lax.fori_loop(0, SW // 8, step, init)
        for c in range(3):
            pair_out[c:c + 1, h * width:(h + 1) * width] = jnp.sum(got[c], axis=0, keepdims=True)

    for c in copies:
        c.wait()


ADJ_ROWS = 192
ALL_ROWS = 240
BLOCK = 256
GHOST_TILES = 8 * LANE_TILES + 4


def fluid_kernel(pops, own, pair, halo_x, halo_y, halo_c, lists, starts_hbm, next_out, force_out,
                 pv, out_v, starts, node, ucat, force, plane, ghosts, cols, pop_sem, out_sem, start_sem):
    loads = [pltpu.make_async_copy(pops.at[q], pv.at[q], pop_sem.at[q]) for q in range(19)]
    start_copy = pltpu.make_async_copy(starts_hbm, starts, start_sem)
    start_copy.start()
    for c in loads:
        c.start()

    start_copy.wait()
    ghosts[...] = jnp.zeros(ghosts.shape, F32)
    lane = lax.broadcasted_iota(jnp.int32, (8, 128), 1)
    sub = lax.broadcasted_iota(jnp.int32, (8, 128), 0)
    total = jnp.int32(0)
    for d, lo, hi in RANGES:
        a = starts[d, 0, lo].astype(jnp.int32)
        b = starts[d, 0, hi].astype(jnp.int32)
        base = total
        sx, sy = SIDES[d]
        moved = jnp.where(sub == 0, float(sx * CX), jnp.where(sub == 1, float(sy * CY), 0.0))

        def put(t, carry, d=d, a=a, b=b, base=base, moved=moved):
            to = base - a + t * 128 + 128 * 8
            by = to & 127
            tile = lax.shift_right_logical(to, 7) - 8
            at = t * 128 + lane
            v = jnp.where((at >= a) & (at < b), lists[d, t] + moved, 0.0)
            v = pltpu.roll(v, by, 1)
            upper = lane >= by
            low = jnp.maximum(tile, 0)
            ghosts[low] = ghosts[low] + jnp.where(upper & (tile >= 0), v, 0.0)
            ghosts[tile + 1] = ghosts[tile + 1] + jnp.where(upper, 0.0, v)
            return carry

        @pl.when(b > a)
        def _(a=a, b=b, put=put):
            lax.fori_loop(lax.shift_right_logical(a, 7), lax.shift_right_logical(b + 127, 7), put, 0)

        total = total + (b - a)

    for c in loads:
        c.wait()
    rho, m = moments(lambda q: pv[q])
    inv = 1.0 / rho
    node[0] = rho
    node[1] = inv
    for c in range(3):
        u = m[c] * inv
        node[2 + c] = u
        corner = []
        for i in range(4):
            for j in range(4):
                sx, sy = (0 if i < 2 else 1), (0 if j < 2 else 1)
                fx, fy = i in (0, 3), j in (0, 3)
                k = 2 * sx + sy
                r = (11 if fy else 8) if fx else (5 if fy else 1)
                corner.append(halo_c[k, r + c:r + c + 1])
        rows = jnp.concatenate(
            [u, halo_x[0, 1 + c], halo_x[1, 1 + c], halo_y[0, 1 + c], halo_y[1, 1 + c]] + corner
            + [halo_x[0, 4 + c], halo_x[1, 4 + c], halo_y[0, 4 + c], halo_y[1, 4 + c]], axis=0)
        hi, lo = split2(rows)
        ucat[c * ALL_ROWS:(c + 1) * ALL_ROWS, 0:128] = hi
        ucat[c * ALL_ROWS:(c + 1) * ALL_ROWS, 128:256] = lo

    force[...] = jnp.zeros(force.shape, F32)
    zi = lax.broadcasted_iota(jnp.int32, (NZ, 1), 0).astype(F32)
    x8 = lax.broadcasted_iota(jnp.int32, (CX, 1), 0).astype(F32)
    y16 = lax.broadcasted_iota(jnp.int32, (CY, 1), 0).astype(F32)
    ki = lax.broadcasted_iota(jnp.int32, (16, 1), 0)
    ii, jj = lax.shift_right_logical(ki, 2), ki & 3
    xd = jnp.where(ii < 2, ii - 2, ii + CX - 2).astype(F32)
    yd = jnp.where(jj < 2, jj - 2, jj + CY - 2).astype(F32)

    def block(vals, live):
        px, py, pz = vals[0:1], vals[1:2], vals[2:3]
        tz = tent(zi - pz)
        zh, zl = split2(tz)
        tx, ty = tent(x8 - px), tent(y16 - py)
        parts = [tx[i:i + 1] * ty for i in range(CX)]
        parts += [tent(-1.0 - px) * ty, tent(CX - px) * ty, tent(-1.0 - py) * tx, tent(CY - py) * tx]
        parts += [tent(xd - px) * tent(yd - py)]
        parts += [tent(-2.0 - px) * ty, tent(CX + 1.0 - px) * ty, tent(-2.0 - py) * tx, tent(CY + 1.0 - py) * tx]
        plane[...] = jnp.concatenate(parts, axis=0)
        zz = jnp.concatenate([zh, zh], axis=0)
        zhl = jnp.concatenate([zh, zl], axis=0)
        sampled = []
        for c in range(3):
            uc = ucat[c * ALL_ROWS:(c + 1) * ALL_ROWS]
            got = dot(uc, zz) + dot(uc[:, :128], zl)
            sampled.append(jnp.sum(got * plane[...], axis=0, keepdims=True))
        for c in range(3):
            react = (vals[3 + c:4 + c] - 2.0 * sampled[c]) * live
            wh, wl = split2(plane[0:ADJ_ROWS] * react)
            both = dot_t(wh, zhl)
            force[c] = force[c] + (both[:, :128] + both[:, 128:] + dot_t(wl, zh))
        return sampled

    for s in range(SW // BLOCK):
        cut = slice(s * BLOCK, (s + 1) * BLOCK)
        vals = own[:, cut]
        got = block(vals, vals[6:7])
        for c in range(3):
            force_out[c:c + 1, cut] = 2.0 * got[c] - vals[3 + c:4 + c] + 0.24 * pair[c:c + 1, cut]

    slot = lax.broadcasted_iota(jnp.int32, (1, BLOCK), 1)

    def ghost_block(i, carry):
        vals = jnp.concatenate([ghosts[2 * i], ghosts[2 * i + 1]], axis=1)
        live = (slot + i * BLOCK < total).astype(F32)
        block(vals, live)
        return carry

    lax.fori_loop(0, lax.shift_right_logical(total + BLOCK - 1, 8), ghost_block, 0)

    slot1 = lax.broadcasted_iota(jnp.int32, (8, 128), 1)

    def ghost_pairs(t, carry):
        g = ghosts[t]
        g = jnp.where((sub == 0) & (slot1 + t * 128 >= total), FAR, g)
        gt = jnp.transpose(g)
        for c in range(3):
            cols[c] = jnp.broadcast_to(gt[:, c:c + 1], (128, 128))
        groups = jnp.minimum(lax.shift_right_logical(total - t * 128 + 7, 3), 16)
        width = 512
        for h in range(SW // width):
            cut = slice(h * width, (h + 1) * width)
            mine = [jnp.broadcast_to(own[c:c + 1, cut], (8, width)) for c in range(3)]

            def step(n, acc, mine=mine):
                at = pl.multiple_of(n * 8, 8)
                p = [jnp.concatenate([cols[c, pl.ds(at, 8)]] * (width // 128), axis=1) for c in range(3)]
                f = pair_terms(*mine, *p)
                return tuple(a + b for a, b in zip(acc, f))

            init = tuple(jnp.zeros((8, width), F32) for _ in range(3))
            got = lax.fori_loop(0, groups, step, init)
            for c in range(3):
                force_out[c:c + 1, cut] = force_out[c:c + 1, cut] + 0.24 * jnp.sum(got[c], axis=0, keepdims=True)
        return carry

    lax.fori_loop(0, lax.shift_right_logical(total + 127, 7), ghost_pairs, 0)
    force_out[...] = force_out[...] * own[6:7]

    def prepare(rho, u0, half, g):
        u = [u0[c] + half * g[c] for c in range(3)]
        uu = u[0] * u[0] + u[1] * u[1] + u[2] * u[2]
        ug = u[0] * g[0] + u[1] * g[1] + u[2] * g[2]
        k0 = 1.25 * rho * (1.0 - 1.5 * uu) - 1.125 * ug
        return k0, 3.75 * rho, 5.625 * rho, u, [1.125 * v for v in g]

    def along(q, v):
        out = None
        for c in range(3):
            s = DIRS[q][c]
            if s:
                out = (v[c] if s > 0 else -v[c]) if out is None else (out + v[c] if s > 0 else out - v[c])
        return out

    def post(q, f, prep):
        k0, r1, r2, u, g = prep
        if q == 0:
            return -0.25 * f + WEIGHTS[0] * k0
        a, p = along(q, u), along(q, g)
        return -0.25 * f + WEIGHTS[q] * (k0 + a * (r1 + r2 * a + 3.0 * p) + p)

    def side_prep(rho, u0, lo, n):
        g = [force[c, lo:lo + n] for c in range(3)]
        return prepare(rho, u0, 0.5 / rho, g)

    inner = side_prep(node[0], [node[2 + c] for c in range(3)], 0, ROWS)
    k0, r1, r2, u, g = inner
    node[1] = k0
    for c in range(3):
        node[2 + c] = u[c]
        node[5 + c] = g[c]
    xs = [side_prep(halo_x[s, 0], [halo_x[s, 1 + c] for c in range(3)], ROWS + s * CY, CY) for s in range(2)]
    ys = [side_prep(halo_y[s, 0], [halo_y[s, 1 + c] for c in range(3)], ROWS + 2 * CY + s * CX, CX)
          for s in range(2)]
    cs = []
    for i in range(4):
        sx, sy = SIDES[4 + i]
        r = ADJ_ROWS - 16 + (1 if sx < 0 else 2) * 4 + (1 if sy < 0 else 2)
        cs.append(side_prep(halo_c[i, 0:1], [halo_c[i, 1 + c:2 + c] for c in range(3)], r, 1))
    stores = []
    for q in range(19):
        dx, dy, dz = DIRS[q]
        rho_q = node[0]
        prep = (node[1], 3.75 * rho_q, 5.625 * rho_q, [node[2 + c] for c in range(3)], [node[5 + c] for c in range(3)])

        def turned(v, dz=dz):
            return pltpu.roll(v, dz % NZ, 1) if dz else v

        v = turned(post(q, pv[q], prep))
        if dy:
            v = pltpu.roll(v, dy % ROWS, 0)
        if dx == 0:
            out_v[q] = v
        else:
            s = 0 if dx > 0 else 1
            e = turned(post(q, halo_x[s, 7 + facing(0, dx).index(q)], xs[s]))
            if dy:
                e = pltpu.roll(e, dy % CY, 0)
            if dx > 0:
                out_v[q, CY:ROWS] = v[0:ROWS - CY]
                out_v[q, 0:CY] = e
            else:
                out_v[q, 0:ROWS - CY] = v[CY:ROWS]
                out_v[q, ROWS - CY:ROWS] = e
        if dy:
            s = 0 if dy > 0 else 1
            at = 0 if dy > 0 else CY - 1
            e = turned(post(q, halo_y[s, 7 + facing(1, dy).index(q)], ys[s]))
            if dx:
                e = pltpu.roll(e, dx % CX, 0)
            out_v[q, pl.ds(at, CX, stride=CY)] = e
            if dx:
                i = SIDES.index((-dx, -dy)) - 4
                r = at + (0 if dx > 0 else (CX - 1) * CY)
                out_v[q, r:r + 1] = post(q, halo_c[i, 4:5], cs[i])
        c = pltpu.make_async_copy(out_v.at[q], next_out.at[q], out_sem.at[q])
        c.start()
        stores.append(c)
    for c in stores:
        c.wait()


def body(n_gx, n_gy, populations, anchor, offsets, heading, velocity, live_count):
    pops = populations.reshape(19, ROWS, NZ)
    vmem = pl.BlockSpec(memory_space=pltpu.VMEM)
    smem = pl.BlockSpec(memory_space=pltpu.SMEM)
    hbm = pl.BlockSpec(memory_space=pl.ANY)
    dma = pltpu.SemaphoreType.DMA
    halo = (
        jax.ShapeDtypeStruct((2, 12, CY, 128), F32),
        jax.ShapeDtypeStruct((2, 12, CX, 128), F32),
        jax.ShapeDtypeStruct((4, 16, 128), F32),
        jax.ShapeDtypeStruct((8, LANE_TILES, 8, 128), F32),
        jax.ShapeDtypeStruct((8, 8, 128), F32),
        jax.ShapeDtypeStruct((8, SW), F32),
        jax.ShapeDtypeStruct((3, SW), F32),
    )
    halo_x, halo_y, halo_c, lists, starts, own, pair = pl.pallas_call(
        functools.partial(exchange_kernel, n_gx, n_gy),
        out_shape=halo,
        in_specs=[hbm, vmem, vmem, vmem, vmem, smem],
        out_specs=[vmem] * 7,
        scratch_shapes=[
            pltpu.VMEM((19, ROWS, NZ), F32),
            pltpu.VMEM((2, 12, CY, 128), F32),
            pltpu.VMEM((2, 12, CX, 128), F32),
            pltpu.VMEM((4, 16, 128), F32),
            pltpu.VMEM((LANE_TILES, 8, 128), F32),
            pltpu.VMEM((8, 128), F32),
            pltpu.VMEM((4, ROWS, NZ), F32),
            pltpu.VMEM((3, SW, 128), F32),
            dma((19,)), dma((24,)), dma((24,)),
        ],
        compiler_params=pltpu.CompilerParams(collective_id=0, has_side_effects=True),
        name="exchange",
    )(pops, anchor, offsets, heading, velocity, live_count)
    moved, force = pl.pallas_call(
        fluid_kernel,
        out_shape=(jax.ShapeDtypeStruct((19, ROWS, NZ), F32), jax.ShapeDtypeStruct((3, SW), F32)),
        in_specs=[hbm, vmem, vmem, vmem, vmem, vmem, vmem, hbm],
        out_specs=[hbm, vmem],
        scratch_shapes=[
            pltpu.VMEM((19, ROWS, NZ), F32),
            pltpu.VMEM((19, ROWS, NZ), F32),
            pltpu.SMEM((8, 8, 128), F32),
            pltpu.VMEM((8, ROWS, NZ), F32),
            pltpu.VMEM((3 * ALL_ROWS, 256), BF16),
            pltpu.VMEM((3, ADJ_ROWS, NZ), F32),
            pltpu.VMEM((ALL_ROWS, BLOCK), F32),
            pltpu.VMEM((GHOST_TILES, 8, 128), F32),
            pltpu.VMEM((3, 128, 128), F32),
            dma((19,)), dma((19,)), dma,
        ],
        name="fluid",
    )(pops, own, pair, halo_x, halo_y, halo_c, lists, starts)
    return (moved.reshape(populations.shape), force.reshape(1, 1, 3, SW))


def solution(mesh):
    return jax.shard_map(
        functools.partial(body, mesh.shape["gx"], mesh.shape["gy"]),
        mesh=mesh,
        in_specs=(
            P(None, "gx", "gy", None),
            P("gx", "gy", None),
            P("gx", "gy", None, None),
            P("gx", "gy", None, None),
            P("gx", "gy", None, None),
            P("gx", "gy"),
        ),
        out_specs=(P(None, "gx", "gy", None), P("gx", "gy", None, None)),
        check_vma=False,
    )
```

time: 166 us -> 45.7 us (0.28)
  the two profiles are of different devices: /device:TPU:304 before, /device:TPU:64 now
where the time goes in v1:
time: 45.7 us; the launch traced here: 45.4 us
  Pallas kernels  40.1 us (88%)
  local copies, waits for them, and re-layouts  3.96 us (9%)
  between operations  1.29 us (3%)
    pallas_call x1, Pallas kernels, body(): pl.pallas_call(functools.partial(exchange_kernel, n_gx, n_gy), out_shape=...  27.5 us
    pallas_call x1, Pallas kernels, body(): pl.pallas_call(fluid_kernel, out_shape=(jax.ShapeDtypeStruct((19, ROWS, N...  12.6 us
    unnamed x3, local copies, waits for them, and re-layouts  3.96 us

profile of v1, /device:TPU:64, one launch (start us, length us, event | category | flops | bytes accessed | tf_op | source)
XLA Modules:
  0.0 45.4 jit_solution(679809203817446909)
XLA Ops:
  1.3 1.3 %copy.8.offsets = f32[1,1,3,1024]{3,2,1,0:T(4,128)} copy(f32[1,1,3,1024]{3,1,2,0:T(1,128)} %param.8) | data formatting | bytes 24576 | tf_op args[2]
  2.6 1.3 %copy.9.velocity = f32[1,1,3,1024]{3,2,1,0:T(4,128)} copy(f32[1,1,3,1024]{3,1,2,0:T(1,128)} %param.10) | data formatting | bytes 24576 | tf_op args[4]
  3.9 27.5 %exchange.1 = (f32[2,12,16,128]{3,2,1,0:T(8,128)}, f32[2,12,8,128]{3,2,1,0:T(8,128)}, f32[4,16,128]{2,1,0:T(8,128)}, f32[8,8,8,128]{3,2,1,0:T(8,128)}, f32[8,8,1...) custom-call(f32[19,128,128]{2,1,0:T(8,128)} %bitcast.3, s32[1,1,1024]{2,1,0:T(1,128)} %anchor.1, ...), custom_call_target="tpu_custom_call" | custom-call | tf_op jit(solution)/shard_map/exchange/pallas_call | solution.py:496
  31.5 12.6 %fluid.1 = (f32[19,128,128]{2,1,0:T(8,128)}, f32[3,1024]{1,0:T(4,128)}) custom-call(f32[19,128,128]{2,1,0:T(8,128)} %bitcast.4, f32[8,1024]{1,0:T(8,128)} %get-tuple-element.11.own, f32[3,1024]{1,0:T(4,128)} %get-tuple-element.12.pair, f32[2,12,16,128]{3,2,1,0:T(8,128)} %get-tuple-element.13.halo_x, f32[2,12,8,128]{3,2,1,0:T(8,128)} %get-tuple-element.14.halo_y, ...), custom_call_target="tpu_custom_call" | custom-call | tf_op jit(solution)/shard_map/fluid/pallas_call | solution.py:515
  44.0 1.3 %copy.10 = f32[1,1,3,1024]{3,1,2,0:T(1,128)} copy(f32[1,1,3,1024]{3,2,1,0:T(4,128)} %bitcast.5) | data formatting | bytes 24576
